TPU v7x, 256 devices: a whole 4x4x8 slice. The times are simulated.
256 devices in a mesh: row: 8 (over x, y_lo), col: 32 (over z, y_hi, core).
Axes of the slice: x: 4, y: 4 (y_hi: 2, y_lo: 2; y = y_hi * 2 + y_lo), z: 8, core: 2. Of those that a mesh axis runs over, the one named last changes fastest.
Arguments:
- grad_out: bfloat16 [2048, 8192], P('col', 'row'), may hold values from -6 to 6
- weight: bfloat16 [28672, 8192], P('col', 'row'), may hold values from -0.0625 to 0.0625
Outputs:
- grad_in: bfloat16 [2048, 28672], P('row', 'col')
All inputs are finite; a program needn't handle non-finite values.
Results may differ from a plain program's by a relative error of at most 0.001.
Values may be sent and summed in bfloat16 or wider, within the bound.
A program may use at most 64 MiB of HBM per device.

v0:
```python
import jax
import jax.numpy as jnp
from jax import lax
from jax.sharding import Mesh
from jax.sharding import PartitionSpec as P

ROW = ("row_0", "row_1")


def scatter_axes(array, axes, dim):
    if not axes:
        return array
    nearer = lax.psum_scatter(array, axes[0], scatter_dimension=dim, tiled=True)
    return scatter_axes(nearer, axes[1:], dim)


def contract(rows_block, weight):
    return lax.dot_general(
        rows_block, weight, (((1,), (1,)), ((), ())), preferred_element_type=jnp.float32
    )


def local(grad_out, weight):
    partial_value = contract(lax.all_gather(grad_out, "col", axis=0, tiled=True), weight)
    return scatter_axes(partial_value, ROW, 0).astype(jnp.bfloat16)


def solution(mesh):
    finer = Mesh(mesh.devices.reshape(4, 2, mesh.shape["col"]), ("row_0", "row_1", "col"))
    in_specs = (P("col", ROW), P("col", ROW))
    out_specs = P(ROW, "col")
    return jax.shard_map(local, mesh=finer, in_specs=in_specs, out_specs=out_specs, check_vma=False)
```

profile of v0, /device:TPU:1, one launch (start us, length us, event | category | flops | bytes accessed | tf_op | source)
XLA Modules:
  0.0 226.0 jit_solution(12876038008683448927)
XLA Ops:
  6.5 0.0 copy-start
  6.5 0.0 all-gather.2.cloned.1.call-start
  6.5 0.7 all-gather.2.cloned.1.call-update
  7.3 0.0 reduce-scatter.3.cloned.1.call-start
  7.3 93.6 %all-gather.2.cloned.1.call-done = bf16[2048,1024]{1,0:T(8,128)(2,1)} async-done(((bf16[64,1024]{1,0:T(8,128)(2,1)}), bf16[2048,1024]{1,0:T(8,128)(2,1)}) %all-gather.2.cloned.1.call-update) | async-done | bytes 4194320 | tf_op jit(solution)/shard_map/all_gather | solution.py:24
  100.9 0.0 copy-done
  100.9 8.8 %fusion = f32[2048,896]{1,0:T(8,128)} fusion(bf16[2048,1024]{1,0:T(8,128)(2,1)} %all-gather.2.cloned.1.call-done, bf16[896,1024]{1,0:T(8,128)(2,1)S(1)} %copy-done), kind=kOutput, calls=%fused_computation | convolution fusion | flops 3758096384 | bytes 13369344 | tf_op jit(solution)/shard_map/dot_general | solution.py:18
  109.7 0.0 reduce-scatter.3.cloned.1.call-update
  109.7 0.0 reduce-scatter.5.cloned.1.call-start
  109.7 71.4 %reduce-scatter.3.cloned.1.call-done = f32[512,896]{1,0:T(8,128)} async-done(((f32[2048,896]{1,0:T(8,128)}), f32[512,896]{1,0:T(8,128)}) %reduce-scatter.3.cloned.1.call-update) | async-done | bytes 1835024 | tf_op jit(solution)/shard_map/reduce_scatter | solution.py:13
  181.2 0.0 reduce-scatter.5.cloned.1.call-update
  181.2 36.3 %reduce-scatter.5.cloned.1.call-done = f32[256,896]{1,0:T(8,128)} async-done(((f32[512,896]{1,0:T(8,128)}), f32[256,896]{1,0:T(8,128)}) %reduce-scatter.5.cloned.1.call-update) | async-done | bytes 917520 | tf_op jit(solution)/shard_map/reduce_scatter | solution.py:13
  217.5 2.0 convert_element_type.3
Async XLA Ops:
  6.5 94.4 %copy-start = (bf16[896,1024]{1,0:T(8,128)(2,1)S(1)}, bf16[896,1024]{1,0:T(8,128)(2,1)}, u32[]{:S(2)}) copy-start(bf16[896,1024]{1,0:T(8,128)(2,1)} %param.3) | copy-start | bytes 5505028
  6.5 94.4 %all-gather.2.cloned.1.call-start = ((), (), s32[]{:S(2)}) async-start(), calls=%async_computation.2 | async-start | bytes 4325376 | tf_op jit(solution)/shard_map/all_gather | solution.py:24
  7.3 173.9 %reduce-scatter.3.cloned.1.call-start = ((), (), s32[]{:S(2)}) async-start(), calls=%async_computation.3 | async-start | bytes 9175040 | tf_op jit(solution)/shard_map/reduce_scatter | solution.py:13
  109.7 107.8 %reduce-scatter.5.cloned.1.call-start = ((), (), s32[]{:S(2)}) async-start(), calls=%async_computation.4 | async-start | bytes 2752512 | tf_op jit(solution)/shard_map/reduce_scatter | solution.py:13
Sparse Core Ops, SparseCore 0:
  10.1 90.7 all-gather.1
  109.8 71.3 reduce-scatter.2
  183.7 33.7 reduce-scatter.4
where the time goes:
time: 226 us
  waiting for transfers between devices  202 us (89%)
  between operations  13.1 us (6%)
  matrix products  8.75 us (4%)
    reduce_scatter x2, waiting for transfers between devices, scatter_axes(): nearer = lax.psum_scatter(array, axes[0], scatter_dimension=dim, tiled=True)  108 us
    all_gather x1, waiting for transfers between devices, local(): lax.all_gather(grad_out, 'col', axis=0, tiled=True)  93.6 us
    dot_general x1, matrix products, contract(): lax.dot_general(rows_block, weight, (((1,), (1,)), ((), ())), preferred_e...  8.75 us
  transfers between devices with their start and end apart: 3, of which 3 were waited for; matrix products, arithmetic and copies ran while one was open for 0% of the time, Pallas kernels for 0%

commit v1 on v0

--- a/solution.py
+++ b/solution.py
@@ -21,7 +21,12 @@
 
 
 def local(grad_out, weight):
-    partial_value = contract(lax.all_gather(grad_out, "col", axis=0, tiled=True), weight)
+    partial_value = contract(
+        jnp.concatenate(
+            lax.all_to_all(jnp.stack([grad_out] * lax.axis_size("col")), "col", 0, 0), axis=0
+        ),
+        weight,
+    )
     return scatter_axes(partial_value, ROW, 0).astype(jnp.bfloat16)
 
 

time: 226 us -> 240 us (1.062)
  blocking collectives: 0 us -> 108 us
  waiting for transfers between devices: 202 us -> 108 us
    all_to_all x0 -> x1, blocking collectives: none -> 108 us  [local(): lax.all_to_all(jnp.stack([grad_out] * lax.axis_size('col')), 'col', 0, 0)]
    all_gather x1 -> x0, waiting for transfers between devices: 93.6 us -> none  [local(): lax.all_gather(grad_out, 'col', axis=0, tiled=True)]
  transfers between devices with their start and end apart: 3 -> 2, of which waited for: 3 -> 2; matrix products, arithmetic and copies ran while one was open for 0% -> 0% of each run, Pallas kernels for 0% -> 0%
where the time goes in v1:
time: 240 us
  blocking collectives  108 us (45%)
  waiting for transfers between devices  108 us (45%)
  between operations  13.4 us (6%)
  matrix products  6.59 us (3%)
    reduce_scatter x2, waiting for transfers between devices, scatter_axes(): nearer = lax.psum_scatter(array, axes[0], scatter_dimension=dim, tiled=True)  108 us
    all_to_all x1, blocking collectives, local(): lax.all_to_all(jnp.stack([grad_out] * lax.axis_size('col')), 'col', 0, 0)  108 us
    dot_general x1, matrix products, contract(): lax.dot_general(rows_block, weight, (((1,), (1,)), ((), ())), preferred_e...  6.59 us
  transfers between devices with their start and end apart: 2, of which 2 were waited for; matrix products, arithmetic and copies ran while one was open for 0% of the time, Pallas kernels for 0%

profile of v1, /device:TPU:1, one launch (start us, length us, event | category | flops | bytes accessed | tf_op | source)
XLA Modules:
  0.0 239.9 jit_solution(14339221556456197767)
XLA Ops:
  6.5 0.0 copy-start
  6.5 0.0 reduce-scatter.3.cloned.1.call-start
  6.5 1.6 stack.2
  8.1 108.0 %all_to_all.5 = bf16[32,64,1024]{2,1,0:T(8,128)(2,1)S(1)} all-to-all(bf16[32,64,1024]{2,1,0:T(8,128)(2,1)S(1)} %stack.2), channel_id=1, replica_groups=mesh['row_0'=4,'row_1'=2,'col'=32] {'col'}, dimensions={0} | all-to-all | bytes 8388608 | tf_op jit(solution)/shard_map/all_to_all | solution.py:26
  116.1 0.0 copy-done
  116.1 6.6 %fusion = f32[2048,896]{1,0:T(8,128)} fusion(bf16[2048,1024]{1,0:T(8,128)(2,1)S(1)} %bitcast.3, bf16[896,1024]{1,0:T(8,128)(2,1)S(1)} %copy-done), kind=kOutput, calls=%fused_computation | convolution fusion | flops 3758096384 | bytes 13369344 | tf_op jit(solution)/shard_map/dot_general | solution.py:18
  122.7 0.0 reduce-scatter.3.cloned.1.call-update
  122.7 0.0 reduce-scatter.5.cloned.1.call-start
  122.8 72.0 %reduce-scatter.3.cloned.1.call-done = f32[512,896]{1,0:T(8,128)} async-done(((f32[2048,896]{1,0:T(8,128)}), f32[512,896]{1,0:T(8,128)}) %reduce-scatter.3.cloned.1.call-update) | async-done | bytes 1835024 | tf_op jit(solution)/shard_map/reduce_scatter | solution.py:13
  194.8 0.0 reduce-scatter.5.cloned.1.call-update
  194.8 36.3 %reduce-scatter.5.cloned.1.call-done = f32[256,896]{1,0:T(8,128)} async-done(((f32[512,896]{1,0:T(8,128)}), f32[256,896]{1,0:T(8,128)}) %reduce-scatter.5.cloned.1.call-update) | async-done | bytes 917520 | tf_op jit(solution)/shard_map/reduce_scatter | solution.py:13
  231.1 2.0 convert_element_type.3
Async XLA Ops:
  6.5 109.6 %copy-start = (bf16[896,1024]{1,0:T(8,128)(2,1)S(1)}, bf16[896,1024]{1,0:T(8,128)(2,1)}, u32[]{:S(2)}) copy-start(bf16[896,1024]{1,0:T(8,128)(2,1)} %param.3) | copy-start | bytes 5505028
  6.5 188.3 %reduce-scatter.3.cloned.1.call-start = ((), (), s32[]{:S(2)}) async-start(), calls=%async_computation.3 | async-start | bytes 9175040 | tf_op jit(solution)/shard_map/reduce_scatter | solution.py:13
  122.7 108.4 %reduce-scatter.5.cloned.1.call-start = ((), (), s32[]{:S(2)}) async-start(), calls=%async_computation.4 | async-start | bytes 2752512 | tf_op jit(solution)/shard_map/reduce_scatter | solution.py:13
Sparse Core Ops, SparseCore 0:
  122.9 71.8 reduce-scatter.2
  197.3 33.7 reduce-scatter.4
